TPU v7x, 256 devices: a whole 4x4x8 slice. The times are simulated.
256 devices in a mesh: blk: 16 (over y_hi, x, core), member: 16 (over z, y_lo).
Axes of the slice: x: 4, y: 4 (y_hi: 2, y_lo: 2; y = y_hi * 2 + y_lo), z: 8, core: 2. Of those that a mesh axis runs over, the one named last changes fastest.
Arguments:
- coords: float32 [16384, 64], P(('blk', 'member')), may hold values from -6 to 6
- codes: int32 [16384, 16, 1024], P('blk', 'member'), may hold values from 0 to 255
- classes: int32 [16384, 16, 1024], P('blk', 'member'), may hold values from 0 to 3
Outputs:
- final_coords: float32 [16384, 64], P(('blk', 'member'))
All inputs are finite; a program needn't handle non-finite values.
Results may differ from a plain program's by a relative error of at most 0.0003.
Values sent between devices are 32-bit elements; how exact they have to be, the bound alone decides.
No kernel may reach another device: no remote copies, remote signals or barrier semaphores. Data moves between devices by JAX's collectives and lax.ppermute only.
A program may use at most 64 MiB of HBM per device.

v0:
```python
import jax
import jax.numpy as jnp
from jax import lax
from jax.sharding import PartitionSpec as P

ITERS = 3


code_step = 0.1
epsilon = 1e-06


def joined_along(parts, dim):
    parts = jnp.moveaxis(parts, 0, dim)
    dims = parts.shape
    return parts.reshape(*dims[:dim], dims[dim] * dims[dim + 1], *dims[dim + 2 :])


def from_everyone(value, axis):
    copies = jnp.broadcast_to(value, (lax.axis_size(axis), *value.shape))
    return lax.all_to_all(copies, axis, split_axis=0, concat_axis=0, tiled=True)


def gathered_copies(value, axis, dim):
    return joined_along(from_everyone(value, axis), dim)


def in_blocks(value, dim, length):
    dims = value.shape
    parts = value.reshape(*dims[:dim], length, dims[dim] // length, *dims[dim + 1 :])
    return jnp.moveaxis(parts, dim, 0)


def sum_at_owner(value, axis, dim):
    parts = in_blocks(value, dim, lax.axis_size(axis))
    arrived = lax.all_to_all(parts, axis, split_axis=0, concat_axis=0, tiled=True)
    return arrived.sum(axis=0)


def side_by_side(arrays, axis, dim, along):
    columns = [a.reshape(*a.shape[:along], -1) for a in arrays]
    both = jnp.concatenate(columns, axis=along)
    out, at, outs = (sum_at_owner(both, axis, dim), 0, [])
    for a, column in zip(arrays, columns):
        piece = out[..., at : at + column.shape[along]]
        outs.append(piece.reshape(*piece.shape[:along], *a.shape[along:]))
        at += column.shape[along]
    return tuple(outs)


def body(coords, codes, classes):
    rows_dev = coords.shape[0]
    n_blocks = lax.axis_size("blk")
    n_members = lax.axis_size("member")
    band_len = rows_dev * n_members
    slab = rows_dev * n_blocks
    blk_index = lax.axis_index("blk")
    mem_index = lax.axis_index("member")
    code_tile = codes.reshape(band_len, slab)
    class_tile = classes.reshape(band_len, slab)
    row_ids = blk_index * band_len + lax.broadcasted_iota(jnp.int32, (band_len, slab), 0)
    col_pos = lax.broadcasted_iota(jnp.int32, (band_len, slab), 1)
    col_ids = col_pos // rows_dev * band_len + mem_index * rows_dev + col_pos % rows_dev
    self_pair = row_ids == col_ids
    weights = jnp.where(self_pair, jnp.float32(0.0), 1.0 / (1.0 + class_tile.astype(jnp.float32)))
    targeted = weights * (code_tile.astype(jnp.float32) + 1.0) * code_step
    weight_rows = jnp.sum(weights, axis=1)
    own_rows = coords
    band = coords
    for step in range(ITERS):
        band = gathered_copies(own_rows, "member", 0)
        columns = gathered_copies(own_rows, "blk", 0)
        gram = jnp.dot(band, columns.T, precision=lax.Precision.HIGHEST)
        dist_sq = (
            jnp.sum(band * band, axis=1)[:, None]
            + jnp.sum(columns * columns, axis=1)[None, :]
            - 2.0 * gram
        )
        dist_sq = jnp.where(self_pair, jnp.float32(1.0), dist_sq)
        ratio = targeted / jnp.sqrt(dist_sq + epsilon)
        numer = jnp.dot(weights - ratio, columns, precision=lax.Precision.HIGHEST)
        numer, ratio_rows = (numer, jnp.sum(ratio, axis=1))
        numer, ratio_rows, weight_own = side_by_side(
            (numer, ratio_rows, weight_rows), "member", 0, 1
        )
        own_rows = (numer + own_rows * ratio_rows[:, None]) / weight_own[:, None]
    return own_rows


def solution(mesh):
    in_specs = (P(("blk", "member"), None), P("blk", "member", None), P("blk", "member", None))
    out_specs = P(("blk", "member"), None)
    return jax.shard_map(body, mesh=mesh, in_specs=in_specs, out_specs=out_specs, check_vma=False)
```

profile of v0, /device:TPU:2, one launch (start us, length us, event | category | flops | bytes accessed | tf_op | source)
XLA Modules:
  0.0 216.8 jit_solution(10989797272185215695)
XLA Ops:
  0.0 0.8 copy.36
  0.9 1.0 reshape.93
  1.9 7.5 %all-to-all-start.1 = ((f32[16,1,4096]{2,1,0:T(1,128)}), f32[16,1,4096]{2,1,0:T(1,128)S(1)}, u32[]{:S(2)}, u32[]{:S(2)}) async-start(f32[16,1,4096]{2,1,0:T(1,128)} %reshape.93), calls=%async_computation.1 | async-start | bytes 524288 | tf_op jit(solution)/shard_map/all_to_all | solution.py:21
  9.4 1.0 reshape.91
  10.5 5.8 %all-to-all-done.1 = f32[16,1,4096]{2,1,0:T(1,128)S(1)} async-done(((f32[16,1,4096]{2,1,0:T(1,128)}), f32[16,1,4096]{2,1,0:T(1,128)S(1)}, u32[]{:S(2)}, u32[]{:S(2)}) %all-to-all-start.1) | async-done | bytes 262176 | tf_op jit(solution)/shard_map/all_to_all | solution.py:21
  16.3 8.7 %all-to-all-start = ((f32[16,1,4096]{2,1,0:T(1,128)}), f32[16,1,4096]{2,1,0:T(1,128)S(1)}, u32[]{:S(2)}, u32[]{:S(2)}) async-start(f32[16,1,4096]{2,1,0:T(1,128)} %reshape.91), calls=%async_computation | async-start | bytes 524288 | tf_op jit(solution)/shard_map/all_to_all | solution.py:21
  25.0 0.5 broadcast.95
  25.5 1.3 reduce.19
  26.8 0.2 reshape.94
  27.0 0.3 copy.38
  27.4 0.2 reshape.79
  27.9 10.6 %all-to-all-done = f32[16,1,4096]{2,1,0:T(1,128)S(1)} async-done(((f32[16,1,4096]{2,1,0:T(1,128)}), f32[16,1,4096]{2,1,0:T(1,128)S(1)}, u32[]{:S(2)}, u32[]{:S(2)}) %all-to-all-start) | async-done | bytes 262176 | tf_op jit(solution)/shard_map/all_to_all | solution.py:21
  38.4 1.3 reduce.18
  39.7 0.2 reshape.92
  40.0 0.3 copy.37
  40.4 0.2 reshape.73
  40.5 11.1 %fusion.15 = (f32[1024]{0:T(1024)S(1)}, f32[1024,1024]{1,0:T(8,128)}, f32[1024]{0:T(1024)S(1)}) fusion(s32[1024,1,1024]{2,1,0:T(1,128)} %param.5, s32[1024]{0:T(1024)S(1)} %get-tuple-element.22, s32[1024]{0:T(1024)S(1)} %get-tuple-element.23, pred[1024]{0:T(1024)(128)(4,1)S(1)} %get-tuple-element.25, s32[]{:T(128)S(6)} %mul.87, ...), kind=kOutput, calls=%fused_computation.46 | convolution fusion | flops 829421568 | bytes 13146116 | tf_op jit(solution)/shard_map/dot_general | solution.py:73
  51.6 0.3 concatenate.30
  52.0 0.3 concatenate.27
  52.3 5.3 %fusion.17 = f32[16,64,64]{2,1,0:T(8,128)S(1)} fusion(f32[16,64,1024]{2,1,0:T(8,128)} %bitcast.90, f32[1024,64,1]{0,1,2:T(8,128)S(1)} %reshape.79), kind=kOutput, calls=%fused_computation.54 | convolution fusion | flops 805306368 | bytes 4718592 | tf_op jit(solution)/shard_map/dot_general | solution.py:81
  57.7 0.3 maximum_maximum_fusion
  58.0 19.4 %all_to_all.45 = f32[16,64,66]{2,1,0:T(8,128)S(1)} all-to-all(f32[16,64,66]{2,1,0:T(8,128)S(1)} %maximum_maximum_fusion), channel_id=1, replica_groups=mesh['blk'=16,'member'=16] {'member'}, dimensions={0} | all-to-all | bytes 540672 | tf_op jit(solution)/shard_map/all_to_all | solution.py:36
  77.5 0.2 slice_reduce_fusion.5
  77.9 1.0 reshape.97
  79.0 5.2 %all-to-all-start.4 = ((f32[16,1,4096]{2,1,0:T(1,128)}), f32[16,1,4096]{2,1,0:T(1,128)S(1)}, u32[]{:S(2)}, u32[]{:S(2)}) async-start(f32[16,1,4096]{2,1,0:T(1,128)} %reshape.97), calls=%async_computation.4 | async-start | bytes 524288 | tf_op jit(solution)/shard_map/all_to_all | solution.py:21
  84.2 1.0 reshape.95
  85.2 5.8 %all-to-all-done.4 = f32[16,1,4096]{2,1,0:T(1,128)S(1)} async-done(((f32[16,1,4096]{2,1,0:T(1,128)}), f32[16,1,4096]{2,1,0:T(1,128)S(1)}, u32[]{:S(2)}, u32[]{:S(2)}) %all-to-all-start.4) | async-done | bytes 262176 | tf_op jit(solution)/shard_map/all_to_all | solution.py:21
  91.0 3.5 %all-to-all-start.3 = ((f32[16,1,4096]{2,1,0:T(1,128)}), f32[16,1,4096]{2,1,0:T(1,128)S(1)}, u32[]{:S(2)}, u32[]{:S(2)}) async-start(f32[16,1,4096]{2,1,0:T(1,128)} %reshape.95), calls=%async_computation.3 | async-start | bytes 524288 | tf_op jit(solution)/shard_map/all_to_all | solution.py:21
  94.6 1.3 reduce.21
  95.9 0.2 reshape.98
  96.1 0.3 copy.43
  96.4 0.2 reshape.80
  96.9 11.3 %all-to-all-done.3 = f32[16,1,4096]{2,1,0:T(1,128)S(1)} async-done(((f32[16,1,4096]{2,1,0:T(1,128)}), f32[16,1,4096]{2,1,0:T(1,128)S(1)}, u32[]{:S(2)}, u32[]{:S(2)}) %all-to-all-start.3) | async-done | bytes 262176 | tf_op jit(solution)/shard_map/all_to_all | solution.py:21
  108.2 1.3 reduce.20
  109.5 0.2 reshape.96
  109.9 0.3 copy.42
  110.2 0.2 reshape.75
  110.4 10.6 %fusion.14 = (f32[1024,1024]{1,0:T(8,128)}, f32[1024]{0:T(1024)S(1)}) fusion(s32[1024,1,1024]{2,1,0:T(1,128)} %param.5, s32[1024]{0:T(1024)S(1)} %get-tuple-element.22, s32[1024]{0:T(1024)S(1)} %get-tuple-element.23, pred[1024]{0:T(1024)(128)(4,1)S(1)} %get-tuple-element.25, s32[]{:T(128)S(6)} %mul.87, s32[1024]{0:T(1024)S(1)} %get-tuple-element.21, ...), kind=kOutput, calls=%fused_computation.45 | convolution fusion | flops 828374016 | bytes 13142020 | tf_op jit(solution)/shard_map/dot_general | solution.py:73
  121.0 0.3 concatenate.28
  121.3 5.4 %fusion.18 = f32[16,64,64]{2,1,0:T(8,128)S(1)} fusion(f32[16,64,1024]{2,1,0:T(8,128)} %bitcast.91, f32[1024,64,1]{0,1,2:T(8,128)S(1)} %reshape.80), kind=kOutput, calls=%fused_computation.55 | convolution fusion | flops 805306368 | bytes 4718592 | tf_op jit(solution)/shard_map/dot_general | solution.py:81
  126.7 0.3 maximum_maximum_fusion.1
  127.1 20.2 %all_to_all.46 = f32[16,64,66]{2,1,0:T(8,128)S(1)} all-to-all(f32[16,64,66]{2,1,0:T(8,128)S(1)} %maximum_maximum_fusion.1), channel_id=1, replica_groups=mesh['blk'=16,'member'=16] {'member'}, dimensions={0} | all-to-all | bytes 540672 | tf_op jit(solution)/shard_map/all_to_all | solution.py:36
  147.3 0.2 slice_reduce_fusion.3
  147.7 1.0 reshape.101
  148.8 3.9 %all-to-all-start.7 = ((f32[16,1,4096]{2,1,0:T(1,128)}), f32[16,1,4096]{2,1,0:T(1,128)S(1)}, u32[]{:S(2)}, u32[]{:S(2)}) async-start(f32[16,1,4096]{2,1,0:T(1,128)} %reshape.101), calls=%async_computation.7 | async-start | bytes 524288 | tf_op jit(solution)/shard_map/all_to_all | solution.py:21
  152.7 1.0 reshape.99
  153.8 5.9 %all-to-all-done.7 = f32[16,1,4096]{2,1,0:T(1,128)S(1)} async-done(((f32[16,1,4096]{2,1,0:T(1,128)}), f32[16,1,4096]{2,1,0:T(1,128)S(1)}, u32[]{:S(2)}, u32[]{:S(2)}) %all-to-all-start.7) | async-done | bytes 262176 | tf_op jit(solution)/shard_map/all_to_all | solution.py:21
  159.7 3.8 %all-to-all-start.6 = ((f32[16,1,4096]{2,1,0:T(1,128)}), f32[16,1,4096]{2,1,0:T(1,128)S(1)}, u32[]{:S(2)}, u32[]{:S(2)}) async-start(f32[16,1,4096]{2,1,0:T(1,128)} %reshape.99), calls=%async_computation.6 | async-start | bytes 524288 | tf_op jit(solution)/shard_map/all_to_all | solution.py:21
  163.4 1.3 reduce.23
  164.7 0.2 reshape.102
  164.9 0.3 copy.48
  165.2 0.2 reshape.81
  165.7 10.5 %all-to-all-done.6 = f32[16,1,4096]{2,1,0:T(1,128)S(1)} async-done(((f32[16,1,4096]{2,1,0:T(1,128)}), f32[16,1,4096]{2,1,0:T(1,128)S(1)}, u32[]{:S(2)}, u32[]{:S(2)}) %all-to-all-start.6) | async-done | bytes 262176 | tf_op jit(solution)/shard_map/all_to_all | solution.py:21
  176.2 1.3 reduce.22
  177.5 0.2 reshape.100
  177.9 0.3 copy.47
  178.2 0.2 reshape.77
  178.4 10.6 %fusion.13 = (f32[1024,1024]{1,0:T(8,128)}, f32[1024]{0:T(1024)S(1)}) fusion(s32[1024,1,1024]{2,1,0:T(1,128)} %param.5, s32[1024]{0:T(1024)S(1)} %get-tuple-element.22, s32[1024]{0:T(1024)S(1)} %get-tuple-element.23, pred[1024]{0:T(1024)(128)(4,1)S(1)} %get-tuple-element.25, s32[]{:T(128)S(6)} %mul.87, s32[1024]{0:T(1024)S(1)} %get-tuple-element.21, ...), kind=kOutput, calls=%fused_computation.44 | convolution fusion | flops 828374016 | bytes 13142020 | tf_op jit(solution)/shard_map/dot_general | solution.py:73
  189.0 0.3 concatenate.29
  189.3 5.3 %fusion.19 = f32[16,64,64]{2,1,0:T(8,128)S(1)} fusion(f32[16,64,1024]{2,1,0:T(8,128)} %bitcast.89, f32[1024,64,1]{0,1,2:T(8,128)S(1)} %reshape.81), kind=kOutput, calls=%fused_computation.56 | convolution fusion | flops 805306368 | bytes 4718592 | tf_op jit(solution)/shard_map/dot_general | solution.py:81
  194.7 0.3 maximum_maximum_fusion.2
  195.0 20.9 %all_to_all.47 = f32[16,64,66]{2,1,0:T(8,128)S(1)} all-to-all(f32[16,64,66]{2,1,0:T(8,128)S(1)} %maximum_maximum_fusion.2), channel_id=1, replica_groups=mesh['blk'=16,'member'=16] {'member'}, dimensions={0} | all-to-all | bytes 540672 | tf_op jit(solution)/shard_map/all_to_all | solution.py:36
  215.9 0.2 slice_reduce_fusion.1
  216.1 0.7 fusion.4
  (34 shorter events, 2.1 us)
Async XLA Ops:
  1.9 14.4 %all-to-all-start.1 = ((f32[16,1,4096]{2,1,0:T(1,128)}), f32[16,1,4096]{2,1,0:T(1,128)S(1)}, u32[]{:S(2)}, u32[]{:S(2)}) async-start(f32[16,1,4096]{2,1,0:T(1,128)} %reshape.93), calls=%async_computation.1 | async-start | bytes 524288 | tf_op jit(solution)/shard_map/all_to_all | solution.py:21
  16.3 22.1 %all-to-all-start = ((f32[16,1,4096]{2,1,0:T(1,128)}), f32[16,1,4096]{2,1,0:T(1,128)S(1)}, u32[]{:S(2)}, u32[]{:S(2)}) async-start(f32[16,1,4096]{2,1,0:T(1,128)} %reshape.91), calls=%async_computation | async-start | bytes 524288 | tf_op jit(solution)/shard_map/all_to_all | solution.py:21
  52.3 25.4 %copy-start = (f32[64,64]{1,0:T(8,128)S(1)}, f32[64,64]{1,0:T(8,128)}, u32[]{:S(2)}) copy-start(f32[64,64]{1,0:T(8,128)} %param.3) | copy-start | bytes 49156
  79.0 12.1 %all-to-all-start.4 = ((f32[16,1,4096]{2,1,0:T(1,128)}), f32[16,1,4096]{2,1,0:T(1,128)S(1)}, u32[]{:S(2)}, u32[]{:S(2)}) async-start(f32[16,1,4096]{2,1,0:T(1,128)} %reshape.97), calls=%async_computation.4 | async-start | bytes 524288 | tf_op jit(solution)/shard_map/all_to_all | solution.py:21
  91.0 17.2 %all-to-all-start.3 = ((f32[16,1,4096]{2,1,0:T(1,128)}), f32[16,1,4096]{2,1,0:T(1,128)S(1)}, u32[]{:S(2)}, u32[]{:S(2)}) async-start(f32[16,1,4096]{2,1,0:T(1,128)} %reshape.95), calls=%async_computation.3 | async-start | bytes 524288 | tf_op jit(solution)/shard_map/all_to_all | solution.py:21
  148.8 10.9 %all-to-all-start.7 = ((f32[16,1,4096]{2,1,0:T(1,128)}), f32[16,1,4096]{2,1,0:T(1,128)S(1)}, u32[]{:S(2)}, u32[]{:S(2)}) async-start(f32[16,1,4096]{2,1,0:T(1,128)} %reshape.101), calls=%async_computation.7 | async-start | bytes 524288 | tf_op jit(solution)/shard_map/all_to_all | solution.py:21
  159.7 16.6 %all-to-all-start.6 = ((f32[16,1,4096]{2,1,0:T(1,128)}), f32[16,1,4096]{2,1,0:T(1,128)S(1)}, u32[]{:S(2)}, u32[]{:S(2)}) async-start(f32[16,1,4096]{2,1,0:T(1,128)} %reshape.99), calls=%async_computation.6 | async-start | bytes 524288 | tf_op jit(solution)/shard_map/all_to_all | solution.py:21
where the time goes:
time: 218 us; the launch traced here: 217 us
  blocking collectives  60.5 us (28%)
  waiting for transfers between devices  49.9 us (23%)
  matrix products  48.4 us (22%)
  starting transfers between devices  32.6 us (15%)
  local copies, waits for them, and re-layouts  14.9 us (7%)
  other arithmetic  10.1 us (5%)
    all_to_all x3, blocking collectives, sum_at_owner(): lax.all_to_all(parts, axis, split_axis=0, concat_axis=0, tiled=True)  60.5 us
    all_to_all x6, waiting for transfers between devices, from_everyone(): return lax.all_to_all(copies, axis, split_axis=0, concat_axis=0, tiled=True)  49.9 us
    all_to_all x6, starting transfers between devices, from_everyone(): return lax.all_to_all(copies, axis, split_axis=0, concat_axis=0, tiled=True)  32.6 us
    dot_general x3, matrix products, body(): gram = jnp.dot(band, columns.T, precision=lax.Precision.HIGHEST)  32.3 us
    dot_general x3, matrix products, body(): numer = jnp.dot(weights - ratio, columns, precision=lax.Precision.HIGHEST)  16.1 us
    unnamed x21, local copies, waits for them, and re-layouts  8.54 us
    all_to_all x6, other arithmetic, from_everyone(): return lax.all_to_all(copies, axis, split_axis=0, concat_axis=0, tiled=True)  7.66 us
  transfers between devices with their start and end apart: 6, of which 6 were waited for; matrix products, arithmetic and copies ran while one was open for 5% of the time, Pallas kernels for 0%

commit v1 on v0

v1 whole, which is shorter than its diff:
```python
import functools

import jax
import jax.numpy as jnp
from jax import lax
from jax.experimental import pallas as pl
from jax.experimental.pallas import tpu as pltpu
from jax.sharding import PartitionSpec as P

ITERS = 3
CODE_STEP = 0.1
EPSILON = 1e-06

D = 64
LANES = 128
F32, BF16 = jnp.float32, jnp.bfloat16
MIB = 1024 * 1024
VMEM = pl.BlockSpec(memory_space=pltpu.VMEM)
SMEM = pl.BlockSpec(memory_space=pltpu.SMEM)


def lanes_of(shape):
    return lax.broadcasted_iota(jnp.int32, shape, len(shape) - 1)


def prepare_kernel(place, codes, classes, weights, targeted, sums):
    band, slab = weights.shape
    per_row = slab // LANES
    blk, mem = place[0], place[1]
    shape = (8, LANES)
    lane = lanes_of(shape)
    sublane = lax.broadcasted_iota(jnp.int32, shape, 0)
    group = lane // 16

    def one_member(member, _):
        tile = jnp.zeros(shape, F32)
        for g in range(D // 8):
            top = pl.multiple_of(member * D + g * 8, 8)
            total = jnp.zeros(shape, F32)
            for c in range(per_row):
                where = pl.ds(top * per_row + c, 8, stride=per_row)
                code = codes[where, :].astype(F32)
                kind = classes[where, :].astype(F32)
                column = lane + c * LANES - blk * D
                own = (sublane + (top - mem * D) == column) & (column >= 0) & (column < D)
                w = jnp.where(own, 0.0, 1.0 / (1.0 + kind))
                cols = slice(c * LANES, (c + 1) * LANES)
                weights[pl.ds(top, 8), cols] = w
                targeted[pl.ds(top, 8), cols] = w * (code + 1.0) * CODE_STEP
                total = total + w
            tile = jnp.where(group == g, jnp.sum(total, axis=1, keepdims=True), tile)
        sums[member] = tile
        return 0

    lax.fori_loop(0, band // D, one_member, 0)


def prepare(place, codes, classes):
    band, slab = codes.shape[0], codes.shape[-1]
    flat = (band * slab // LANES, LANES)
    return pl.pallas_call(
        prepare_kernel,
        out_shape=(
            jax.ShapeDtypeStruct((band, slab), F32),
            jax.ShapeDtypeStruct((band, slab), F32),
            jax.ShapeDtypeStruct((band // D, 8, LANES), F32),
        ),
        in_specs=[SMEM, VMEM, VMEM],
        out_specs=(VMEM, VMEM, VMEM),
        name="prepare",
        compiler_params=pltpu.CompilerParams(vmem_limit_bytes=20 * MIB),
        cost_estimate=pl.CostEstimate(flops=10**7, bytes_accessed=16 * MIB, transcendentals=0),
    )(place, codes.reshape(flat), classes.reshape(flat))


def split3(x):
    a = x.astype(BF16).astype(F32)
    rest = x - a
    b = rest.astype(BF16).astype(F32)
    return a, b, rest - b


def operand(y, lane, column):
    left = lane < D
    hi = y.astype(BF16).astype(F32)
    lo = (y - hi).astype(BF16).astype(F32)
    square = (hi + lo) * (hi + lo)
    hi_other, lo_other = pltpu.roll(hi, D, 1), pltpu.roll(lo, D, 1)
    halves = []
    for half in range(2):
        norm = jnp.sum(jnp.where(left == (half == 0), square, 0.0), axis=1, keepdims=True)
        if column:
            norm = norm + EPSILON
        a, b, c = split3(jnp.broadcast_to(norm, y.shape))
        h = (hi, hi_other)[half]
        if column:
            extra = jnp.where(lane == 69, c, 0.0)
            extra = jnp.where(lane == 68, b, extra)
            extra = jnp.where(lane == 67, a, extra)
            extra = jnp.where(lane < 67, 1.0, extra)
            first = -2.0 * jnp.where(left, h, (lo_other, lo)[half])
            second = jnp.where(left, -2.0 * h, extra)
        else:
            extra = jnp.where(lane < 70, 1.0, 0.0)
            extra = jnp.where(lane == 66, c, extra)
            extra = jnp.where(lane == 65, b, extra)
            extra = jnp.where(lane == 64, a, extra)
            first = jnp.where(left, h, (hi_other, hi)[half])
            second = jnp.where(left, (lo, lo_other)[half], extra)
        halves.append((first.astype(BF16), second.astype(BF16)))
    return halves


def step_kernel(chunk, rows_ref, columns_ref, weights, targeted, sums, out, left_op, right_op):
    members, packed, _ = rows_ref.shape
    lane = lanes_of((packed, LANES))
    left = lane < D
    for m in range(members):
        for ref, dst, column in ((rows_ref, left_op, False), (columns_ref, right_op, True)):
            for half, (first, second) in enumerate(operand(ref[m], lane, column)):
                at = m * D + half * packed
                dst[at : at + packed, :LANES] = first
                dst[at : at + packed, LANES:] = second
    band, slab = weights.shape
    for c in range(band // chunk):
        rows = slice(c * chunk, (c + 1) * chunk)
        a = left_op[rows, :]
        acc = jnp.zeros((chunk, 2 * LANES), F32)
        for n in range(slab // 256):
            cols = slice(n * 256, (n + 1) * 256)
            b = right_op[cols, :]
            dist_sq = lax.dot_general(a, b, (((1,), (1,)), ((), ())), preferred_element_type=F32)
            gap = weights[rows, cols] - targeted[rows, cols] * lax.rsqrt(jnp.maximum(dist_sq, EPSILON))
            hi = gap.astype(BF16)
            lo = (gap - hi.astype(F32)).astype(BF16)
            acc = acc + jnp.dot(hi, b, preferred_element_type=F32)
            acc = acc + jnp.dot(lo, b, preferred_element_type=F32)
        pulled = acc[:, :LANES]
        pulled = -0.5 * (pulled + pltpu.roll(pulled, D, 1))
        total = jnp.broadcast_to(acc[:, LANES + D : LANES + D + 1], (chunk, LANES))
        for k in range(chunk // D):
            m = c * (chunk // D) + k
            y = rows_ref[m]
            lower = slice(k * D, k * D + packed)
            upper = slice(k * D + packed, (k + 1) * D)
            out[m, :packed, :] = jnp.where(left, pulled[lower] - y * total[lower], pulled[upper] - y * total[upper])
    if out.shape[1] > packed:
        out[:, packed:, :] = sums[...]


def step(rows, columns, weights, targeted, sums, with_sums):
    members, packed, _ = rows.shape
    band, slab = weights.shape
    return pl.pallas_call(
        functools.partial(step_kernel, 256),
        out_shape=jax.ShapeDtypeStruct((members, packed + (8 if with_sums else 0), LANES), F32),
        in_specs=[VMEM] * 5,
        out_specs=VMEM,
        scratch_shapes=[pltpu.VMEM((band, 2 * LANES), BF16), pltpu.VMEM((slab, 2 * LANES), BF16)],
        name="step",
        compiler_params=pltpu.CompilerParams(vmem_limit_bytes=16 * MIB),
        cost_estimate=pl.CostEstimate(flops=2 * 10**9, bytes_accessed=9 * MIB, transcendentals=MIB),
    )(rows, columns, weights, targeted, sums)


def sum_of(parts):
    return functools.reduce(jnp.add, [parts[m] for m in range(parts.shape[0])])


def update_kernel(first, last, parts, own, scale, *outs):
    packed = own.shape[0]
    lane = lanes_of((packed, LANES))
    left = lane < D
    if first:
        tile = sum_of(parts.at[:, packed:, :])
        halves = []
        for half in range(2):
            groups = [half * 4 + k for k in range(packed // 8)]
            halves.append(jnp.concatenate([jnp.broadcast_to(tile[:, g * 16 : g * 16 + 1], (8, LANES)) for g in groups], axis=0))
        inverse = 1.0 / jnp.where(left, halves[0], halves[1])
        outs[-1][...] = inverse
    else:
        inverse = scale[...]
    moved = own[...] + sum_of(parts.at[:, :packed, :]) * inverse
    if last:
        outs[0][:packed, :] = moved[:, :D]
        outs[0][packed:, :] = pltpu.roll(moved, D, 1)[:, :D]
    else:
        outs[0][...] = moved


def update(parts, own, scale, first, last):
    packed = own.shape[0]
    shape = jax.ShapeDtypeStruct((2 * packed, D) if last else own.shape, F32)
    outs = (shape, jax.ShapeDtypeStruct(own.shape, F32)) if first else (shape,)
    return pl.pallas_call(
        functools.partial(update_kernel, first, last),
        out_shape=outs,
        in_specs=[VMEM] * 3,
        out_specs=(VMEM,) * len(outs),
        name="update",
        compiler_params=pltpu.CompilerParams(vmem_limit_bytes=4 * MIB),
    )(parts, own, scale)


def exchange(parts, axis):
    return lax.all_to_all(parts, axis, split_axis=0, concat_axis=0, tiled=True)


def to_all(value, axis):
    return exchange(jnp.broadcast_to(value, (lax.axis_size(axis), *value.shape)), axis)


def body(coords, codes, classes):
    packed = coords.shape[0] // 2
    place = jnp.stack([lax.axis_index("blk"), lax.axis_index("member")]).astype(jnp.int32)
    own = jnp.concatenate([coords[:packed], coords[packed:]], axis=1)
    weights, targeted, sums = prepare(place, codes, classes)
    scale = own
    for at in range(ITERS):
        columns = to_all(own, "blk")
        rows = to_all(own, "member")
        parts = step(rows, columns, weights, targeted, sums, at == 0)
        outs = update(exchange(parts, "member"), own, scale, at == 0, at == ITERS - 1)
        own = outs[0]
        if at == 0:
            scale = outs[1]
    return own


def solution(mesh):
    in_specs = (P(("blk", "member"), None), P("blk", "member", None), P("blk", "member", None))
    out_specs = P(("blk", "member"), None)
    return jax.shard_map(body, mesh=mesh, in_specs=in_specs, out_specs=out_specs, check_vma=False)
```

time: 218 us -> 159 us (0.73)
  blocking collectives: 60.5 us -> 119 us
  matrix products: 48.4 us -> 0 us
  waiting for transfers between devices: 49.9 us -> 1.81 us
  starting transfers between devices: 32.6 us -> 8.68 us
  Pallas kernels: 0 us -> 15 us
  other arithmetic: 10.1 us -> 0.15 us
    all_to_all x3 -> x8, blocking collectives: 60.5 us -> 119 us  [exchange(): return lax.all_to_all(parts, axis, split_axis=0, concat_axis=0, tiled=True)]
    dot_general x6 -> x0, matrix products: 48.4 us -> none  [the longest x3 32.3 us: body(): gram = jnp.dot(band, columns.T, precision=lax.Precision.HIGHEST)]
    all_to_all x6 -> x1, waiting for transfers between devices: 49.9 us -> 1.81 us  [exchange(): return lax.all_to_all(parts, axis, split_axis=0, concat_axis=0, tiled=True)]
    all_to_all x6 -> x1, starting transfers between devices: 32.6 us -> 8.68 us  [exchange(): return lax.all_to_all(parts, axis, split_axis=0, concat_axis=0, tiled=True)]
    pallas_call x0 -> x7, Pallas kernels: none -> 15 us  [the longest x3 10.9 us: step(): pl.pallas_call(functools.partial(step_kernel, 256), out_shape=jax.ShapeDt...]
    all_to_all x6 -> x0, other arithmetic: 7.66 us -> none  [from_everyone(): return lax.all_to_all(copies, axis, split_axis=0, concat_axis=0, tiled=True)]
    unnamed x21 -> x12, local copies, waits for them, and re-layouts: 8.54 us -> 12.7 us
    all_to_all x7 -> x0, local copies, waits for them, and re-layouts: 2.36 us -> none  [from_everyone(): return lax.all_to_all(copies, axis, split_axis=0, concat_axis=0, tiled=True)]
  transfers between devices with their start and end apart: 6 -> 1, of which waited for: 6 -> 1; matrix products, arithmetic and copies ran while one was open for 5% -> 0% of each run, Pallas kernels for 0% -> 2%
where the time goes in v1:
time: 159 us
  blocking collectives  119 us (75%)
  Pallas kernels  15 us (9%)
  local copies, waits for them, and re-layouts  14.2 us (9%)
  starting transfers between devices  8.68 us (5%)
  waiting for transfers between devices  1.81 us (1%)
    all_to_all x8, blocking collectives, exchange(): return lax.all_to_all(parts, axis, split_axis=0, concat_axis=0, tiled=True)  119 us
    unnamed x12, local copies, waits for them, and re-layouts  12.7 us
    pallas_call x3, Pallas kernels, step(): pl.pallas_call(functools.partial(step_kernel, 256), out_shape=jax.ShapeDt...  10.9 us
    all_to_all x1, starting transfers between devices, exchange(): return lax.all_to_all(parts, axis, split_axis=0, concat_axis=0, tiled=True)  8.68 us
    pallas_call x1, Pallas kernels, prepare(): pl.pallas_call(prepare_kernel, out_shape=(jax.ShapeDtypeStruct((band, sla...  3.25 us
  transfers between devices with their start and end apart: 1, of which 1 were waited for; matrix products, arithmetic and copies ran while one was open for 0% of the time, Pallas kernels for 2%

profile of v1, /device:TPU:2, one launch (start us, length us, event | category | flops | bytes accessed | tf_op | source)
XLA Modules:
  0.0 158.6 jit_solution(11023940489952910265)
XLA Ops:
  0.0 0.7 fusion
  0.7 0.1 pad_maximum_fusion.own.scale
  0.8 0.8 broadcast_in_dim.12
  1.6 14.3 %all_to_all.45.columns_ref = f32[16,32,128]{2,1,0:T(8,128)S(1)} all-to-all(f32[16,32,128]{2,1,0:T(8,128)} %broadcast_in_dim.12), channel_id=1, replica_groups=mesh['blk'=16,'member'=16] {'blk'}, dimensions={0} | all-to-all | bytes 524288 | tf_op jit(solution)/shard_map/all_to_all | solution.py:207
  15.9 8.7 %all-to-all-start = ((f32[16,32,128]{2,1,0:T(8,128)}), f32[16,32,128]{2,1,0:T(8,128)S(1)}, u32[]{:S(2)}, u32[]{:S(2)}) async-start(f32[16,32,128]{2,1,0:T(8,128)} %broadcast_in_dim.12), calls=%async_computation | async-start | bytes 524288 | tf_op jit(solution)/shard_map/all_to_all | solution.py:207
  24.6 0.1 pad_add_fusion.place
  24.7 0.0 copy-start.4
  24.7 2.2 %copy-done.4 = s32[1024,1,1024]{2,1,0:T(1,128)S(1)} copy-done((s32[1024,1,1024]{2,1,0:T(1,128)S(1)}, s32[1024,1,1024]{2,1,0:T(1,128)}, u32[]{:S(2)}) %copy-start.4) | copy-done | bytes 4194328
  26.9 0.0 copy-start.5
  26.9 2.2 %copy-done.5 = s32[1024,1,1024]{2,1,0:T(1,128)S(1)} copy-done((s32[1024,1,1024]{2,1,0:T(1,128)S(1)}, s32[1024,1,1024]{2,1,0:T(1,128)}, u32[]{:S(2)}) %copy-start.5) | copy-done | bytes 4194328
  29.1 3.2 %prepare.1 = (f32[1024,1024]{1,0:T(8,128)S(1)}, f32[1024,1024]{1,0:T(8,128)S(1)}, f32[16,8,128]{2,1,0:T(8,128)S(1)}) custom-call(s32[2]{0:T(128)S(1)} %pad_add_fusion.place, s32[8192,128]{1,0:T(8,128)S(1)} %bitcast.4, s32[8192,128]{1,0:T(8,128)S(1)} %bitcast.5), custom_call_target="tpu_custom_call" | custom-call | flops 10000000 | bytes 16777216 | tf_op jit(solution)/shard_map/prepare/pallas_call | solution.py:61
  32.3 0.0 copy-start
  32.4 1.9 %copy-done = f32[1024,1024]{1,0:T(8,128)} copy-done((f32[1024,1024]{1,0:T(8,128)}, f32[1024,1024]{1,0:T(8,128)S(1)}, u32[]{:S(2)}) %copy-start) | copy-done | bytes 4194328
  34.3 0.0 copy-start.2
  34.3 2.0 %copy-done.2 = f32[1024,1024]{1,0:T(8,128)} copy-done((f32[1024,1024]{1,0:T(8,128)}, f32[1024,1024]{1,0:T(8,128)S(1)}, u32[]{:S(2)}) %copy-start.2) | copy-done | bytes 4194328
  36.3 1.8 %all-to-all-done.rows_ref = f32[16,32,128]{2,1,0:T(8,128)S(1)} async-done(((f32[16,32,128]{2,1,0:T(8,128)}), f32[16,32,128]{2,1,0:T(8,128)S(1)}, u32[]{:S(2)}, u32[]{:S(2)}) %all-to-all-start) | async-done | bytes 262176 | tf_op jit(solution)/shard_map/all_to_all | solution.py:207
  38.1 0.0 copy-start.1
  38.1 2.2 %copy-done.1 = f32[1024,1024]{1,0:T(8,128)S(1)} copy-done((f32[1024,1024]{1,0:T(8,128)S(1)}, f32[1024,1024]{1,0:T(8,128)}, u32[]{:S(2)}) %copy-start.1) | copy-done | bytes 4194328
  40.3 0.0 copy-start.3
  40.3 2.2 %copy-done.3 = f32[1024,1024]{1,0:T(8,128)S(1)} copy-done((f32[1024,1024]{1,0:T(8,128)S(1)}, f32[1024,1024]{1,0:T(8,128)}, u32[]{:S(2)}) %copy-start.3) | copy-done | bytes 4194328
  42.5 3.6 %step.3 = f32[16,40,128]{2,1,0:T(8,128)S(1)} custom-call(f32[16,32,128]{2,1,0:T(8,128)S(1)} %all-to-all-done.rows_ref, f32[16,32,128]{2,1,0:T(8,128)S(1)} %all_to_all.45.columns_ref, f32[1024,1024]{1,0:T(8,128)S(1)} %copy-done.1, f32[1024,1024]{1,0:T(8,128)S(1)} %copy-done.3, f32[16,8,128]{2,1,0:T(8,128)S(1)} %get-tuple-element.12.sums), custom_call_target="tpu_custom_call" | custom-call | flops 2000000000 | bytes 9437184 | tf_op jit(solution)/shard_map/step/pallas_call | solution.py:154
  46.1 20.0 %all_to_all.46.parts = f32[16,40,128]{2,1,0:T(8,128)S(1)} all-to-all(f32[16,40,128]{2,1,0:T(8,128)S(1)} %step.3), channel_id=1, replica_groups=mesh['blk'=16,'member'=16] {'member'}, dimensions={0} | all-to-all | bytes 655360 | tf_op jit(solution)/shard_map/all_to_all | solution.py:207
  66.1 0.1 update.3
  66.2 11.5 %all_to_all.47.columns_ref = f32[16,32,128]{2,1,0:T(8,128)S(1)} all-to-all(f32[16,32,128]{2,1,0:T(8,128)S(1)} %broadcast_in_dim.13), channel_id=1, replica_groups=mesh['blk'=16,'member'=16] {'blk'}, dimensions={0} | all-to-all | bytes 524288 | tf_op jit(solution)/shard_map/all_to_all | solution.py:207
  77.7 16.3 %all_to_all.48.rows_ref = f32[16,32,128]{2,1,0:T(8,128)S(1)} all-to-all(f32[16,32,128]{2,1,0:T(8,128)S(1)} %broadcast_in_dim.13), channel_id=1, replica_groups=mesh['blk'=16,'member'=16] {'member'}, dimensions={0} | all-to-all | bytes 524288 | tf_op jit(solution)/shard_map/all_to_all | solution.py:207
  94.1 3.6 %step.4 = f32[16,32,128]{2,1,0:T(8,128)S(1)} custom-call(f32[16,32,128]{2,1,0:T(8,128)S(1)} %all_to_all.48.rows_ref, f32[16,32,128]{2,1,0:T(8,128)S(1)} %all_to_all.47.columns_ref, f32[1024,1024]{1,0:T(8,128)S(1)} %copy-done.1, f32[1024,1024]{1,0:T(8,128)S(1)} %copy-done.3, f32[16,8,128]{2,1,0:T(8,128)S(1)} %get-tuple-element.12.sums), custom_call_target="tpu_custom_call" | custom-call | flops 2000000000 | bytes 9437184 | tf_op jit(solution)/shard_map/step/pallas_call | solution.py:154
  97.7 14.3 %all_to_all.49.parts = f32[16,32,128]{2,1,0:T(8,128)S(1)} all-to-all(f32[16,32,128]{2,1,0:T(8,128)S(1)} %step.4), channel_id=1, replica_groups=mesh['blk'=16,'member'=16] {'member'}, dimensions={0} | all-to-all | bytes 524288 | tf_op jit(solution)/shard_map/all_to_all | solution.py:207
  112.1 11.1 %all_to_all.50.columns_ref = f32[16,32,128]{2,1,0:T(8,128)S(1)} all-to-all(f32[16,32,128]{2,1,0:T(8,128)S(1)} %broadcast_in_dim.14), channel_id=1, replica_groups=mesh['blk'=16,'member'=16] {'blk'}, dimensions={0} | all-to-all | bytes 524288 | tf_op jit(solution)/shard_map/all_to_all | solution.py:207
  123.2 16.3 %all_to_all.51.rows_ref = f32[16,32,128]{2,1,0:T(8,128)S(1)} all-to-all(f32[16,32,128]{2,1,0:T(8,128)S(1)} %broadcast_in_dim.14), channel_id=1, replica_groups=mesh['blk'=16,'member'=16] {'member'}, dimensions={0} | all-to-all | bytes 524288 | tf_op jit(solution)/shard_map/all_to_all | solution.py:207
  139.5 3.6 %step.5 = f32[16,32,128]{2,1,0:T(8,128)S(1)} custom-call(f32[16,32,128]{2,1,0:T(8,128)S(1)} %all_to_all.51.rows_ref, f32[16,32,128]{2,1,0:T(8,128)S(1)} %all_to_all.50.columns_ref, f32[1024,1024]{1,0:T(8,128)S(1)} %copy-done.1, f32[1024,1024]{1,0:T(8,128)S(1)} %copy-done.3, f32[16,8,128]{2,1,0:T(8,128)S(1)} %get-tuple-element.12.sums), custom_call_target="tpu_custom_call" | custom-call | flops 2000000000 | bytes 9437184 | tf_op jit(solution)/shard_map/step/pallas_call | solution.py:154
  143.1 14.8 %all_to_all.52.parts = f32[16,32,128]{2,1,0:T(8,128)S(1)} all-to-all(f32[16,32,128]{2,1,0:T(8,128)S(1)} %step.5), channel_id=1, replica_groups=mesh['blk'=16,'member'=16] {'member'}, dimensions={0} | all-to-all | bytes 524288 | tf_op jit(solution)/shard_map/all_to_all | solution.py:207
  157.9 0.7 update.5
  (3 shorter events, 0.1 us)
Async XLA Ops:
  15.9 22.1 %all-to-all-start = ((f32[16,32,128]{2,1,0:T(8,128)}), f32[16,32,128]{2,1,0:T(8,128)S(1)}, u32[]{:S(2)}, u32[]{:S(2)}) async-start(f32[16,32,128]{2,1,0:T(8,128)} %broadcast_in_dim.12), calls=%async_computation | async-start | bytes 524288 | tf_op jit(solution)/shard_map/all_to_all | solution.py:207
  24.7 2.2 %copy-start.4 = (s32[1024,1,1024]{2,1,0:T(1,128)S(1)}, s32[1024,1,1024]{2,1,0:T(1,128)}, u32[]{:S(2)}) copy-start(s32[1024,1,1024]{2,1,0:T(1,128)} %param.4) | copy-start | bytes 12582916
  26.9 2.2 %copy-start.5 = (s32[1024,1,1024]{2,1,0:T(1,128)S(1)}, s32[1024,1,1024]{2,1,0:T(1,128)}, u32[]{:S(2)}) copy-start(s32[1024,1,1024]{2,1,0:T(1,128)} %param.5) | copy-start | bytes 12582916
  32.3 1.9 %copy-start = (f32[1024,1024]{1,0:T(8,128)}, f32[1024,1024]{1,0:T(8,128)S(1)}, u32[]{:S(2)}) copy-start(f32[1024,1024]{1,0:T(8,128)S(1)} %get-tuple-element.10.weights) | copy-start | bytes 12582916
  34.3 2.0 %copy-start.2 = (f32[1024,1024]{1,0:T(8,128)}, f32[1024,1024]{1,0:T(8,128)S(1)}, u32[]{:S(2)}) copy-start(f32[1024,1024]{1,0:T(8,128)S(1)} %get-tuple-element.11.targeted) | copy-start | bytes 12582916
  38.1 2.2 %copy-start.1 = (f32[1024,1024]{1,0:T(8,128)S(1)}, f32[1024,1024]{1,0:T(8,128)}, u32[]{:S(2)}) copy-start(f32[1024,1024]{1,0:T(8,128)} %copy-done) | copy-start | bytes 12582916
  40.3 2.2 %copy-start.3 = (f32[1024,1024]{1,0:T(8,128)S(1)}, f32[1024,1024]{1,0:T(8,128)}, u32[]{:S(2)}) copy-start(f32[1024,1024]{1,0:T(8,128)} %copy-done.2) | copy-start | bytes 12582916
